TPU v7x, 32 devices: a whole 2x2x4 slice. The times are simulated.
32 devices in a mesh: row: 8 (over y, x, core), col: 4 (over z).
Axes of the slice: x: 2, y: 2, z: 4, core: 2. Of those that a mesh axis runs over, the one named last changes fastest.
Arguments:
- tokens: bfloat16 [4096, 2048], P(('row', 'col')), may hold values from -30 to 30
- ln1_gain: float32 [2048], replicated, may hold values from 0.25 to 1.75
- qkv_weight: bfloat16 [2048, 16, 3, 128], P('row', 'col'), may hold values from -4 to 4
- out_weight: bfloat16 [2048, 2048], P('col', 'row'), may hold values from -0.125 to 0.125
- ln2_gain: float32 [2048], replicated, may hold values from 0.25 to 1.75
- ffn_in: bfloat16 [2048, 8192], P('row', 'col'), may hold values from -0.125 to 0.125
- ffn_out: bfloat16 [8192, 2048], P('col', 'row'), may hold values from -0.0625 to 0.0625
- expert_ids: int32 [4096, 1], P(('row', 'col')), may hold values from 0 to 15; in each aligned block of 128 rows (0 to 127, 128 to 255, ...) at most 16 rows name the same one
- expert_in: bfloat16 [32, 2048, 2048], P(('row', 'col')), may hold values from -0.125 to 0.125
- expert_out: bfloat16 [32, 2048, 2048], P(('row', 'col')), may hold values from -0.09375 to 0.09375
Outputs:
- block_out: bfloat16 [4096, 2048], P(('row', 'col'))
Inputs may be any that keep to these rules, and one draw needn't show every extreme that they name: `expert_ids`: among the tokens of one device no expert is named more than 16 times, and in every draw some expert is named exactly 16 times by the tokens of some device.
All inputs are finite; a program needn't handle non-finite values.
Results may differ from a plain program's by a relative error of at most 0.013.
Values may be sent and summed in bfloat16 or wider, within the bound.
A program may use at most 128 MiB of HBM per device.

v0:
```python
import functools
import jax
import jax.numpy as jnp
from jax import lax
from jax.experimental import pallas as pl
from jax.experimental.pallas import tpu as pltpu
from jax.sharding import PartitionSpec as P

MESH = pl.DeviceIdType.MESH


def flipped(index, bit):
    return index + bit - 2 * bit * ((index // bit) % 2)


def comm_body(plan, row_total, col_total, *refs):
    gathers, spreads, sums, shuffles, units = plan
    count = len(gathers) + len(spreads) + len(sums) + len(shuffles)
    ins, refs = refs[:count], refs[count:]
    operands, refs = refs[: 2 * len(units)], refs[2 * len(units) :]
    outs, refs = refs[:count], refs[count:]
    results, refs = refs[: len(units)], refs[len(units) :]
    stages, refs = refs[:count], refs[count:]
    sum_slots = refs[: 2 * len(sums)]
    send, recv, local = refs[2 * len(sums) :]
    row = lax.axis_index("row")
    col = lax.axis_index("col")

    barrier = pltpu.get_barrier_semaphore()
    peers = 0
    if gathers or shuffles:
        for step in range(1, row_total):
            pl.semaphore_signal(
                barrier, inc=1, device_id=(lax.rem(row + step, row_total), col), device_id_type=MESH
            )
            peers += 1
    if spreads or sums:
        for step in range(1, col_total):
            pl.semaphore_signal(
                barrier, inc=1, device_id=(row, lax.rem(col + step, col_total)), device_id_type=MESH
            )
            peers += 1

    loads = []
    for i in range(count):
        load = pltpu.make_async_copy(ins[i], stages[i], local.at[i])
        load.start()
        loads.append(load)
    pl.semaphore_wait(barrier, peers)

    serial = [0]
    finish = []
    pending = []
    kept = []

    def number():
        serial[0] += 1
        return serial[0] - 1

    def remote(k, src, dst, device):
        return pltpu.make_async_remote_copy(
            src, dst, send.at[k], recv.at[k], device_id=device, device_id_type=MESH
        )

    def copy(src, dst, arriving, device):
        k = number()
        out = remote(k, src, dst, device)
        out.start()
        finish.append((None, out))
        return remote(k, src, arriving, device)

    def copy_if(condition, k, src, dst, device):
        out = remote(k, src, dst, device)
        pl.when(condition)(out.start)
        finish.append((condition, out))

    def keep(i, src, dst):
        own = pltpu.make_async_copy(src, dst, local.at[count + i])
        own.start()
        kept.append(own)

    right = (row, lax.rem(col + 1, col_total))
    left = (row, lax.rem(col + col_total - 1, col_total))
    last = col_total - 1
    lines = []
    base = len(gathers)
    for i in range(base, base + len(spreads)):
        loads[i].wait()
        size = ins[i].shape[0]

        def block(index, i=i, size=size):
            index = lax.rem(index + col_total, col_total)
            return outs[i].at[pl.ds(pl.multiple_of(index * size, size), size)]

        keys = [(number(), number()) for _ in range(last)]
        copy_if(col < last, keys[0][0], stages[i], block(col), right)
        copy_if(col > 0, keys[0][1], stages[i], block(col), left)
        keep(i, stages[i], block(col))

        def advance(step, block=block, keys=keys):
            got = block(col - 1 - step)
            pl.when(col > step)(remote(keys[step][0], got, got, right).wait_recv)
            if step + 1 < last:
                copy_if((col > step) & (col < last), keys[step + 1][0], got, got, right)
            got = block(col + 1 + step)
            pl.when(col + step < last)(remote(keys[step][1], got, got, left).wait_recv)
            if step + 1 < last:
                copy_if((col + step < last) & (col > 0), keys[step + 1][1], got, got, left)

        lines.append(advance)
    base += len(spreads)
    for j in range(len(sums)):
        i = base + j
        loads[i].wait()
        stage, total = stages[i], outs[i]
        slots, merged = sum_slots[2 * j], sum_slots[2 * j + 1]
        keys = [number() for _ in range(col_total)]
        merge = col_total >= 4
        if merge:
            key = number()
            copy_if(col == 0, key, stage.at[last], merged, right)
            copy_if(col == last, key, stage.at[0], merged, left)

        def send_block(target, condition, source, stage=stage, slots=slots, keys=keys):
            out = pltpu.make_async_remote_copy(
                source,
                slots.at[col],
                send.at[keys[target]],
                recv.at[keys[0] + col],
                device_id=(row, target),
                device_id_type=MESH,
            )
            pl.when(condition)(out.start)
            finish.append((condition, out))

        for target in range(col_total):
            condition = col != target
            if merge and target == last:
                condition = condition & (col > 1)
            if merge and target == 0:
                condition = condition & (col < last - 1)
            send_block(target, condition, stage.at[target])
        total[...] = stage[pl.ds(col, 1)][0].astype(jnp.float32)

        def combine(stage=stage, merged=merged, key=key if merge else 0, send_block=send_block):
            for target, holder in ((last, 1), (0, last - 1)):
                pl.when(col == holder)(remote(key, merged, merged, right).wait_recv)

                @pl.when(col == holder)
                def _():
                    merged[...] = (
                        merged[...].astype(jnp.float32) + stage[target].astype(jnp.float32)
                    ).astype(merged.dtype)

                send_block(target, col == holder, merged)

        def collect(total=total, slots=slots, keys=keys, merge=merge):
            for source in range(col_total):
                condition = col != source
                if merge and source == 0:
                    condition = condition & (col < last)
                if merge and source == last:
                    condition = condition & (col > 0)
                slot = slots.at[source]
                pl.when(condition)(remote(keys[source], slot, slot, right).wait_recv)

                @pl.when(condition)
                def _():
                    total[...] += slots[source].astype(jnp.float32)

        def advance(step, combine=combine, collect=collect, merge=merge):
            if step == 0 and merge:
                combine()
            if step == last - 1:
                collect()

        lines.append(advance)
    base += len(sums)
    for i in range(base, base + len(shuffles)):
        loads[i].wait()
        for step in range(1, row_total):
            to = lax.rem(row + (step if shuffles[i - base] > 0 else row_total - step), row_total)
            slot = outs[i].at[step]
            pending.append(copy(stages[i].at[step], slot, slot, (to, col)))
        keep(i, stages[i].at[0], outs[i].at[0])

    partner = flipped(row, 1)
    relay = row_total == 8

    def piece(i, index, half):
        depth, width = ins[i].shape
        start, size = (0, depth) if half is None else (half * (depth // 2), depth // 2)
        if gathers[i] == 0:
            return outs[i].at[pl.ds(pl.multiple_of(index * depth + start, size), size)]
        return outs[i].at[pl.ds(start, size), pl.ds(pl.multiple_of(index * width, width), width)]

    arrivals = []
    for i in range(len(gathers)):
        loads[i].wait()
        mine = piece(i, row, None)
        if relay:
            sources = [flipped(row, 2), flipped(row, 4)]
            targets = sources
        else:
            sources = [lax.rem(row + row_total - 2 * d, row_total) for d in range(1, row_total // 2)]
            targets = [lax.rem(row + 2 * d, row_total) for d in range(1, row_total // 2)]
        first = [
            (source, copy(stages[i], mine, piece(i, source, None), (target, col)))
            for source, target in zip(sources, targets)
        ]
        pending.append(copy(stages[i], mine, piece(i, partner, None), (partner, col)))
        keep(i, stages[i], mine)
        arrivals.append(first)

    def hand_on(i, source, half):
        got = piece(i, source, half)
        pending.append(copy(got, got, piece(i, flipped(source, 1), half), (partner, col)))

    seconds = []

    def first_level(i):
        if not relay:
            for source, arrival in arrivals[i]:
                arrival.wait_recv()
                hand_on(i, source, None)
            return
        (by_x, from_x), (by_y, from_y) = arrivals[i]
        across = flipped(by_x, 4)
        from_x.wait_recv()
        got = piece(i, by_x, 0)
        diag_a = copy(got, got, piece(i, across, 0), (by_y, col))
        hand_on(i, by_x, None)
        from_y.wait_recv()
        got = piece(i, by_y, 1)
        diag_b = copy(got, got, piece(i, across, 1), (by_x, col))
        hand_on(i, by_y, None)
        seconds.append((i, across, diag_a, diag_b))

    early = len(gathers) // 2 if lines else 0
    for step in range(last if lines else 0):
        for advance in lines:
            advance(step)
        if step == 0:
            for i in range(early):
                first_level(i)
        if step == min(1, last - 1):
            for i in range(early, len(gathers)):
                first_level(i)
    if not lines:
        for i in range(len(gathers)):
            first_level(i)
    for n in range(len(units)):
        x_ref, w_ref, o_ref = operands[2 * n], operands[2 * n + 1], results[n]
        rows, depth = x_ref.shape
        width = w_ref.shape[1]
        tile = min(width, 256)
        pltpu.emit_pipeline(
            up_body if units[n] else plain_body,
            grid=(width // tile,),
            in_specs=[
                pl.BlockSpec((rows, depth), lambda j: (0, 0)),
                pl.BlockSpec((depth, tile), lambda j: (0, j)),
            ],
            out_specs=[pl.BlockSpec((rows, tile), lambda j: (0, j))],
        )(x_ref, w_ref, o_ref)
    for i, across, diag_a, diag_b in seconds:
        for half, arrival in ((0, diag_a), (1, diag_b)):
            arrival.wait_recv()
            hand_on(i, across, half)
    for arrival in pending:
        arrival.wait_recv()
    for condition, out in finish:
        if condition is None:
            out.wait_send()
        else:
            pl.when(condition)(out.wait_send)
    for own in kept:
        own.wait()


def exchange(name, collective_id, gathers=(), spreads=(), sums=(), shuffles=(), units=()):
    row_total = lax.axis_size("row")
    col_total = lax.axis_size("col")
    arrays, shapes, copies = [], [], 0
    hbm, vmem = pl.BlockSpec(memory_space=pl.ANY), pl.BlockSpec(memory_space=pltpu.VMEM)
    for array, axis in gathers:
        depth, width = array.shape
        arrays.append(array)
        shape = (depth * row_total, width) if axis == 0 else (depth, width * row_total)
        shapes.append((shape, array.dtype, hbm))
        copies += 9 if row_total == 8 else row_total
    for array in spreads:
        arrays.append(array)
        shape = (array.shape[0] * col_total,) + array.shape[1:]
        shapes.append((shape, array.dtype, hbm))
        copies += 2 * (col_total - 1)
    slots = []
    for array in sums:
        arrays.append(array)
        shapes.append((array.shape[1:], jnp.float32, vmem))
        slots += [pltpu.VMEM(array.shape, array.dtype), pltpu.VMEM(array.shape[1:], array.dtype)]
        copies += col_total + 1
    for array, _ in shuffles:
        arrays.append(array)
        shapes.append((array.shape, array.dtype, hbm))
        copies += row_total - 1
    operands = []
    for x, w, _ in units:
        operands += [x, w]
        shapes.append(((x.shape[0], w.shape[1]), jnp.bfloat16, hbm))
    plan = (
        [axis for _, axis in gathers],
        [0] * len(spreads),
        [0] * len(sums),
        [sign for _, sign in shuffles],
        [with_gelu for _, _, with_gelu in units],
    )
    return pl.pallas_call(
        functools.partial(comm_body, plan, row_total, col_total),
        out_shape=[jax.ShapeDtypeStruct(shape, dtype) for shape, dtype, _ in shapes],
        in_specs=[hbm] * (len(arrays) + len(operands)),
        out_specs=[spec for _, _, spec in shapes],
        scratch_shapes=[pltpu.VMEM(a.shape, a.dtype) for a in arrays]
        + slots
        + [
            pltpu.SemaphoreType.DMA((copies,)),
            pltpu.SemaphoreType.DMA((copies,)),
            pltpu.SemaphoreType.DMA((2 * len(arrays),)),
        ],
        compiler_params=pltpu.CompilerParams(
            collective_id=collective_id, has_side_effects=True, vmem_limit_bytes=16 * 2**20
        ),
        name=name,
    )(*arrays, *operands)


def plain_body(x_ref, w_ref, o_ref):
    inner = jnp.dot(x_ref[...], w_ref[...], preferred_element_type=jnp.float32)
    o_ref[...] = inner.astype(o_ref.dtype)


def up_body(x_ref, w_ref, o_ref):
    inner = jnp.dot(x_ref[...], w_ref[...], preferred_element_type=jnp.float32)
    o_ref[...] = (inner * (1.0 + lax.erf(inner * (0.5**0.5))) * 0.5).astype(o_ref.dtype)


def up_gelu(x, w):
    rows, depth = x.shape
    width = w.shape[1]
    tile = min(width, 256)
    return pl.pallas_call(
        up_body,
        grid=(width // tile,),
        out_shape=jax.ShapeDtypeStruct((rows, width), jnp.bfloat16),
        in_specs=[
            pl.BlockSpec((rows, depth), lambda j: (0, 0)),
            pl.BlockSpec((depth, tile), lambda j: (0, j)),
        ],
        out_specs=pl.BlockSpec((rows, tile), lambda j: (0, j)),
        compiler_params=pltpu.CompilerParams(vmem_limit_bytes=32 * 2**20),
        cost_estimate=pl.CostEstimate(
            flops=2 * rows * depth * width,
            bytes_accessed=2 * (rows * depth + depth * width + rows * width),
            transcendentals=0,
        ),
        name="up_gelu",
    )(x, w)


def layer_norm(row_data, gain_vector):
    row_data = row_data.astype(jnp.float32)
    centered = row_data - jnp.mean(row_data, axis=-1, keepdims=True)
    spread = jnp.mean(centered * centered, axis=-1, keepdims=True)
    return centered * lax.rsqrt(spread + 1e-06) * gain_vector


def matmul(a, b):
    return jnp.dot(a, b, preferred_element_type=jnp.float32)


def shards(
    tokens,
    ln1_gain,
    qkv_weight,
    out_weight,
    ln2_gain,
    ffn_in,
    ffn_out,
    expert_ids,
    expert_in,
    expert_out,
):
    tok_count, model_width = tokens.shape
    row_total = lax.axis_size("row")
    col_total = lax.axis_size("col")
    row_index = lax.axis_index("row")
    col_index = lax.axis_index("col")
    expert_count = row_total * col_total // 2
    capacity = max(2, 2 * tok_count // expert_count)
    head_count, head_dim = qkv_weight.shape[1], qkv_weight.shape[3]
    seq_len = tok_count * col_total

    ids_block = jnp.broadcast_to(expert_ids[:, 0][None, :], (8, tok_count))
    qkv_whole, out_whole, image_rows, ids_all = exchange(
        "enter",
        0,
        gathers=((qkv_weight.reshape(qkv_weight.shape[0], -1), 0), (out_weight, 1)),
        spreads=(tokens, ids_block),
    )
    normed = layer_norm(image_rows, ln1_gain).astype(jnp.bfloat16)
    projected = matmul(normed, qkv_whole).astype(jnp.bfloat16)
    projected = projected.reshape(seq_len, head_count, 3, head_dim)
    queries, keys, values = projected[:, :, 0], projected[:, :, 1], projected[:, :, 2]
    scores = jnp.einsum("qhd,khd->hqk", queries, keys, preferred_element_type=jnp.float32)
    scores = scores * (head_dim ** (-0.5))
    weights = jnp.exp(scores - jnp.max(scores, axis=-1, keepdims=True))
    probabilities = (weights / jnp.sum(weights, axis=-1, keepdims=True)).astype(jnp.bfloat16)
    attended = jnp.einsum("hqk,khd->qhd", probabilities, values, preferred_element_type=jnp.float32)
    attended = attended.astype(jnp.bfloat16).reshape(seq_len, head_count * head_dim)
    head_terms = matmul(attended, out_whole).astype(jnp.bfloat16)
    head_terms = head_terms.reshape(col_total, tok_count, model_width)

    up_whole, mixed_heads = exchange("heads", 1, gathers=((ffn_in, 0),), sums=(head_terms,))
    hidden_mine = (tokens.astype(jnp.float32) + mixed_heads).astype(jnp.bfloat16)
    normed_mine = layer_norm(hidden_mine, ln2_gain).astype(jnp.bfloat16)

    down_whole, normed_image = exchange(
        "norms", 2, gathers=((ffn_out, 1),), spreads=(normed_mine,)
    )

    ids_rows = ids_all.reshape(col_total, 8, tok_count)[:, 0]
    expert_range = jnp.arange(expert_count, dtype=jnp.int32)
    one_hot = (ids_rows[:, :, None] == expert_range).astype(jnp.int32)
    earlier = jnp.cumsum(one_hot, axis=1) - one_hot
    slot_index = jnp.sum(earlier * one_hot, axis=2)
    block_index = jnp.arange(col_total, dtype=jnp.int32)[:, None]
    home_row = 2 * ids_rows // col_total
    mine = (2 * ids_rows % col_total) // 2 == col_index // 2
    step = (home_row - row_index + row_total) % row_total
    position = (step * col_total + block_index) * capacity + slot_index
    position = jnp.where(mine, position, -1).reshape(seq_len)
    slot_count = row_total * col_total * capacity
    slots = jnp.arange(slot_count, dtype=jnp.int32)
    placing = (slots[:, None] == position[None, :]).astype(jnp.bfloat16)
    picking = (position[:, None] == slots[None, :]).astype(jnp.bfloat16)

    table = matmul(placing, normed_image).astype(jnp.bfloat16)
    table = table.reshape(row_total, col_total * capacity, model_width)
    expert_rows, hidden_units = exchange(
        "dispatch", 3, shuffles=((table, 1),), units=((normed_image, up_whole, True),)
    )
    expert_units = up_gelu(expert_rows.reshape(slot_count, model_width), expert_in[0])
    partial_out = matmul(expert_units, expert_out[0]).astype(jnp.bfloat16)
    partial_out = partial_out.reshape(row_total, col_total * capacity, model_width)
    returned, dense_part = exchange(
        "collect", 4, shuffles=((partial_out, -1),), units=((hidden_units, down_whole, False),)
    )

    rows_two = returned.reshape(slot_count, model_width)
    partial = dense_part.astype(jnp.float32) + matmul(picking, rows_two)
    partial = partial.astype(jnp.bfloat16).reshape(col_total, tok_count, model_width)
    (total,) = exchange("leave", 5, sums=(partial,))
    return (hidden_mine.astype(jnp.float32) + total).astype(jnp.bfloat16)


def solution(mesh):
    in_specs = (
        P(("row", "col"), None),
        P(),
        P("row", "col", None, None),
        P("col", "row"),
        P(),
        P("row", "col"),
        P("col", "row"),
        P(("row", "col"), None),
        P(("row", "col"), None, None),
        P(("row", "col"), None, None),
    )
    out_specs = P(("row", "col"), None)
    return jax.shard_map(shards, mesh=mesh, in_specs=in_specs, out_specs=out_specs, check_vma=False)
```

profile of v0, /device:TPU:6, one launch (start us, length us, event | category | flops | bytes accessed | tf_op | source)
XLA Modules:
  0.0 260.6 jit_solution(4351793981807558918)
XLA Ops:
  0.0 0.7 broadcast_in_dim.6.refs_3_
  0.7 1.5 copy.16
  2.2 0.3 copy.17.refs_0_
  2.5 0.0 copy-start
  2.5 1.0 copy-done
  3.5 0.9 copy-done.4
  4.5 42.7 %enter.1 = (bf16[2048,1536]{1,0:T(8,128)(2,1)S(1)}, bf16[512,2048]{1,0:T(8,128)(2,1)S(1)}, bf16[512,2048]{1,0:T(8,128)(2,1)S(1)}, s32[32,128]{1,0:T(8,128)S(1)}) custom-call(bf16[256,1536]{1,0:T(8,128)(2,1)S(1)} %copy.17.refs_0_, bf16[512,256]{1,0:T(8,128)(2,1)S(1)} %copy-done.4, bf16[128,2048]{1,0:T(8,128)(2,1)S(1)} %copy-done, ...), custom_call_target="tpu_custom_call" | custom-call | tf_op jit(solution)/shard_map/enter/pallas_call | solution.py:318
  47.2 0.3 convert_reduce_fusion
  47.6 0.7 fusion.5
  48.3 0.0 copy-done.9
  48.3 4.7 %convolution_convert_fusion.2 = bf16[512,1536]{1,0:T(8,128)(2,1)} fusion(bf16[2048,1536]{1,0:T(8,128)(2,1)S(1)} %get-tuple-element.18, bf16[512,2048]{1,0:T(8,128)(2,1)S(1)} %get-tuple-element.17, f32[2048]{0:T(1024)S(1)} %copy-done.9, f32[512]{0:T(512)S(1)} %add_rsqrt_fusion, f32[512]{0:T(512)S(1)} %broadcast_multiply_fusion.1), kind=kOutput, calls=%fused_computation.18 | convolution fusion | flops 3227254784 | bytes 9973760 | tf_op jit(solution)/shard_map/dot_general | solution.py:378
  53.0 2.6 %copy.18 = bf16[512,1536]{0,1:T(8,128)(2,1)} copy(bf16[512,1536]{1,0:T(8,128)(2,1)} %convolution_convert_fusion.2) | data formatting | bytes 3145728 | tf_op jit(solution)/shard_map/convert_element_type | solution.py:411
  55.6 0.1 fusion.30
  55.7 0.3 reduce_window_sum.11
  56.0 0.2 select_reduce_fusion
  56.3 2.0 fusion.27
  58.2 0.0 copy-start.7
  58.3 1.9 copy-done.7
  60.2 1.1 fusion.51
  61.2 5.2 %fusion.20 = bf16[4,128,512]{2,1,0:T(8,128)(2,1)S(1)} fusion(f32[4,512]{1,0:T(4,128)S(1)} %fusion.51, bf16[512,4,3,128]{0,3,2,1:T(8,128)(2,1)} %bitcast.55, f32[4,512,512]{1,2,0:T(8,128)} %copy-done.7), kind=kOutput, calls=%fused_computation.27 | convolution fusion | flops 273943040 | bytes 9445376 | tf_op jit(solution)/shard_map/hqk,khd->qhd/dot_general | solution.py:418
  66.5 0.0 copy-start.2
  66.5 0.0 copy-start.1
  66.5 1.3 convolution_convert_fusion.1
  67.8 0.0 copy-start.8
  67.8 0.0 copy-start.3
  67.8 0.0 copy-done.2
  67.8 41.9 %heads.1 = (bf16[2048,2048]{1,0:T(8,128)(2,1)S(1)}, f32[128,2048]{1,0:T(8,128)S(1)}) custom-call(bf16[256,2048]{1,0:T(8,128)(2,1)S(1)} %copy-done.2, bf16[4,128,2048]{2,1,0:T(8,128)(2,1)S(1)} %bitcast.44), custom_call_target="tpu_custom_call" | custom-call | tf_op jit(solution)/shard_map/heads/pallas_call | solution.py:318
  109.7 0.2 convert_reduce_fusion.1
  110.0 0.3 fusion.23
  110.3 0.0 copy-done.8
  110.3 0.4 fusion.25.refs_1_
  110.6 43.7 %norms.1 = (bf16[2048,2048]{1,0:T(8,128)(2,1)S(1)}, bf16[512,2048]{1,0:T(8,128)(2,1)S(1)}) custom-call(bf16[2048,256]{1,0:T(8,128)(2,1)S(1)} %copy-done.3, bf16[128,2048]{1,0:T(8,128)(2,1)S(1)} %fusion.25.refs_1_), custom_call_target="tpu_custom_call" | custom-call | tf_op jit(solution)/shard_map/norms/pallas_call | solution.py:318
  154.3 0.0 slice-start
  154.3 1.3 convolution_convert_fusion
  155.6 0.0 slice-start.1
  155.6 0.0 slice-start.2
  155.6 24.7 %dispatch.1 = (bf16[8,64,2048]{2,1,0:T(8,128)(2,1)S(1)}, bf16[512,2048]{1,0:T(8,128)(2,1)S(1)}) custom-call(bf16[8,64,2048]{2,1,0:T(8,128)(2,1)S(1)} %bitcast.47, bf16[512,2048]{1,0:T(8,128)(2,1)S(1)} %get-tuple-element.22.refs_1_, bf16[2048,2048]{1,0:T(8,128)(2,1)S(1)} %get-tuple-element.23.refs_2_), custom_call_target="tpu_custom_call" | custom-call | tf_op jit(solution)/shard_map/dispatch/pallas_call | solution.py:318
  180.4 0.0 copy-start.5
  180.4 1.3 copy-done.5
  181.7 1.6 copy-done.6
  183.3 7.2 %up_gelu.1 = bf16[512,2048]{1,0:T(8,128)(2,1)S(1)} custom-call(bf16[512,2048]{1,0:T(8,128)(2,1)S(1)} %bitcast.53, bf16[2048,2048]{1,0:T(8,128)(2,1)S(1)} %bitcast.51), custom_call_target="tpu_custom_call" | custom-call | flops 4294967296 | bytes 12582912 | tf_op jit(solution)/shard_map/up_gelu/pallas_call | solution.py:351
  190.6 0.0 slice-done.2
  190.6 0.0 slice-done.3
  190.6 4.7 %fusion.11 = bf16[512,2048]{1,0:T(8,128)(2,1)S(1)} fusion(bf16[512,2048]{1,0:T(8,128)(2,1)S(1)} %up_gelu.1, bf16[1,2048,2048]{2,1,0:T(8,128)(2,1)S(1)} %bitcast.62), kind=kOutput, calls=%fused_computation.15 | convolution fusion | flops 4296015872 | bytes 12582912 | tf_op jit(solution)/shard_map/dot_general | solution.py:378
  195.3 27.9 %collect.1 = (bf16[8,64,2048]{2,1,0:T(8,128)(2,1)S(1)}, bf16[512,2048]{1,0:T(8,128)(2,1)S(1)}) custom-call(bf16[8,64,2048]{2,1,0:T(8,128)(2,1)S(1)} %bitcast.46, bf16[512,2048]{1,0:T(8,128)(2,1)S(1)} %get-tuple-element.25.refs_1_, bf16[2048,2048]{1,0:T(8,128)(2,1)S(1)} %get-tuple-element.26.refs_2_), custom_call_target="tpu_custom_call" | custom-call | tf_op jit(solution)/shard_map/collect/pallas_call | solution.py:318
  223.2 1.3 add_convert_fusion
  224.6 35.1 %leave.1 = f32[128,2048]{1,0:T(8,128)S(1)} custom-call(bf16[4,128,2048]{2,1,0:T(8,128)(2,1)S(1)} %bitcast.45), custom_call_target="tpu_custom_call" | custom-call | tf_op jit(solution)/shard_map/leave/pallas_call | solution.py:318
  259.7 0.9 fusion.26
  (16 shorter events, 0.1 us)
Async XLA Ops:
  0.7 47.6 %copy-start.9 = (f32[2048]{0:T(1024)S(1)}, f32[2048]{0:T(1024)}, u32[]{:S(2)}) copy-start(f32[2048]{0:T(1024)} %param.11) | copy-start | bytes 24580
  2.5 1.0 copy-start
  3.5 0.9 copy-start.4
  58.2 1.9 copy-start.7
  66.5 1.3 copy-start.2
  66.5 43.2 %copy-start.1 = (bf16[128,2048]{1,0:T(8,128)(2,1)S(1)}, bf16[128,2048]{1,0:T(8,128)(2,1)}, u32[]{:S(2)}) copy-start(bf16[128,2048]{1,0:T(8,128)(2,1)} %refs_2_.1) | copy-start | bytes 1572868
  67.8 42.5 %copy-start.8 = (f32[2048]{0:T(1024)S(1)}, f32[2048]{0:T(1024)}, u32[]{:S(2)}) copy-start(f32[2048]{0:T(1024)} %param.14) | copy-start | bytes 24580
  67.8 42.8 %copy-start.3 = (bf16[2048,256]{1,0:T(8,128)(2,1)S(1)}, bf16[2048,256]{1,0:T(8,128)(2,1)}, u32[]{:S(2)}) copy-start(bf16[2048,256]{1,0:T(8,128)(2,1)} %refs_0_.3) | copy-start | bytes 3145732
  154.3 27.4 %slice-start = ((s8[8388608]{0:T(1024)(128)(4,1)}), s8[4194304]{0:T(1024)(128)(4,1)S(1)}, s32[]{:S(2)}) async-start(s8[8388608]{0:T(1024)(128)(4,1)} %bitcast.49), calls=%async_computation | async-start | bytes 8388608
  155.6 26.1 %slice-start.1 = ((s8[8388608]{0:T(1024)(128)(4,1)}), s8[4194304]{0:T(1024)(128)(4,1)S(1)}, s32[]{:S(2)}) async-start(s8[8388608]{0:T(1024)(128)(4,1)} %bitcast.49), calls=%async_computation.1 | async-start | bytes 8388608
  155.6 34.9 %slice-start.2 = ((s8[8388608]{0:T(1024)(128)(4,1)}), s8[4194304]{0:T(1024)(128)(4,1)S(1)}, s32[]{:S(2)}) async-start(s8[8388608]{0:T(1024)(128)(4,1)} %bitcast.61), calls=%async_computation.2 | async-start | bytes 8388608
  180.4 1.4 copy-start.5
  181.7 1.6 copy-start.6
  183.3 7.3 %slice-start.3 = ((s8[8388608]{0:T(1024)(128)(4,1)}), s8[4194304]{0:T(1024)(128)(4,1)S(1)}, s32[]{:S(2)}) async-start(s8[8388608]{0:T(1024)(128)(4,1)} %bitcast.61), calls=%async_computation.3 | async-start | bytes 8388608
where the time goes:
time: 263 us; the launch traced here: 261 us
  Pallas kernels  223 us (85%)
  matrix products  20.5 us (8%)
  local copies, waits for them, and re-layouts  12 us (5%)
  other arithmetic  4.63 us (2%)
    pallas_call x6, Pallas kernels, exchange(): pl.pallas_call(functools.partial(comm_body, plan, row_total, col_total),...  216 us
    dot_general x5, matrix products, matmul(): return jnp.dot(a, b, preferred_element_type=jnp.float32)  13.3 us
    unnamed x29, local copies, waits for them, and re-layouts  8.44 us
    pallas_call x1, Pallas kernels, up_gelu(): pl.pallas_call(up_body, grid=(width // tile,), out_shape=jax.ShapeDtypeSt...  7.24 us

commit v1 on v0

--- a/solution.py
+++ b/solution.py
@@ -378,6 +378,516 @@
     return jnp.dot(a, b, preferred_element_type=jnp.float32)
 
 
+def chosen(table, index):
+    value = jnp.int32(table[0])
+    for n in range(1, len(table)):
+        value = jnp.where(index == n, jnp.int32(table[n]), value)
+    return value
+
+
+def near_first(total):
+    return [sorted(range(total), key=lambda b: (abs(b - c), b)) for c in range(total)]
+
+
+def far_first(total):
+    return [sorted(range(total), key=lambda b: (-abs(b - c), -b)) for c in range(total)]
+
+
+def block_body(sizes, *refs):
+    row_total, col_total, capacity, heads, parts = sizes
+    (tokens_in, gain_one, gain_two, ids_in, qkv_in, out_in, up_in, down_in, first_in, second_in) = refs[:10]
+    result = refs[10]
+    (tokens, image, fresh, qkv, outw, upw, downw, first, second, proj, attended, stage, slots) = refs[11:24]
+    (own_sum, hidden, table, landed, returned, units, codes) = refs[24:31]
+    (load_sem, ag_send, ag_recv, code_send, code_recv, rs_send, rs_recv) = refs[31:38]
+    (gather_send, gather_recv, out_send, out_recv, back_send, back_recv) = refs[38:]
+    row = lax.axis_index("row")
+    col = lax.axis_index("col")
+    last = col_total - 1
+    tok, model = tokens.shape
+    size = tok // parts
+    head_dim = attended.shape[1] // heads
+    f32 = jnp.float32
+
+    barrier = pltpu.get_barrier_semaphore()
+    for step in range(1, row_total):
+        pl.semaphore_signal(
+            barrier, inc=1, device_id=(lax.rem(row + step, row_total), col), device_id_type=MESH
+        )
+    for step in range(1, col_total):
+        pl.semaphore_signal(
+            barrier, inc=1, device_id=(row, lax.rem(col + step, col_total)), device_id_type=MESH
+        )
+
+    finish = []
+
+    def remote(src, dst, send, recv, device):
+        return pltpu.make_async_remote_copy(
+            src, dst, send, recv, device_id=device, device_id_type=MESH
+        )
+
+    def launch(copy, condition=None, into=None):
+        if condition is None:
+            copy.start()
+        else:
+            pl.when(condition)(copy.start)
+        (finish if into is None else into).append((condition, copy))
+
+    def drain(items):
+        for condition, copy in items:
+            if condition is None:
+                copy.wait_send()
+            else:
+                pl.when(condition)(copy.wait_send)
+        items.clear()
+
+    wholes = [(qkv, qkv_in, 0), (outw, out_in, 1), (upw, up_in, 0), (downw, down_in, 1)]
+
+    def piece(g, index, half=None):
+        whole, part, axis = wholes[g]
+        depth, width = part.shape
+        start, count = (0, depth) if half is None else (half * (depth // 2), depth // 2)
+        if axis == 0:
+            return whole.at[pl.ds(pl.multiple_of(index * depth + start, count), count)]
+        return whole.at[pl.ds(start, count), pl.ds(pl.multiple_of(index * width, width), width)]
+
+    loads = [pltpu.make_async_copy(tokens_in, tokens, load_sem.at[0])]
+    for g in range(4):
+        loads.append(pltpu.make_async_copy(wholes[g][1], piece(g, row), load_sem.at[1 + g]))
+    loads.append(pltpu.make_async_copy(first_in, first, load_sem.at[5]))
+    loads.append(pltpu.make_async_copy(second_in, second, load_sem.at[6]))
+    for load in loads:
+        load.start()
+
+    partner, by_x, by_y = flipped(row, 1), flipped(row, 2), flipped(row, 4)
+    across = flipped(by_x, 4)
+
+    def gather_copy(g, key, index, half, target):
+        part = piece(g, index, half)
+        return remote(part, part, gather_send.at[g, key], gather_recv.at[g, key], (target, col))
+
+    def gather_wait(g, key, index, half=None):
+        gather_copy(g, key, index, half, partner).wait_recv()
+
+    def gather_start(g):
+        loads[1 + g].wait()
+        launch(gather_copy(g, 0, row, None, by_x))
+        launch(gather_copy(g, 1, row, None, by_y))
+        launch(gather_copy(g, 2, row, None, partner))
+
+    def gather_relay(g):
+        gather_wait(g, 0, by_x)
+        launch(gather_copy(g, 3, by_x, 0, by_y))
+        launch(gather_copy(g, 5, by_x, None, partner))
+        gather_wait(g, 1, by_y)
+        launch(gather_copy(g, 4, by_y, 1, by_x))
+        launch(gather_copy(g, 6, by_y, None, partner))
+
+    def gather_finish(g):
+        gather_wait(g, 3, across, 0)
+        launch(gather_copy(g, 7, across, 0, partner))
+        gather_wait(g, 4, across, 1)
+        launch(gather_copy(g, 8, across, 1, partner))
+
+    def gather_complete(g):
+        gather_wait(g, 2, partner)
+        gather_wait(g, 5, flipped(by_x, 1))
+        gather_wait(g, 6, flipped(by_y, 1))
+        gather_wait(g, 7, flipped(across, 1), 0)
+        gather_wait(g, 8, flipped(across, 1), 1)
+
+    near = [chosen([order[k] for order in near_first(col_total)], col) for k in range(col_total)]
+    far = [chosen([order[k] for order in far_first(col_total)], col) for k in range(col_total)]
+
+    def rows_of(h):
+        return pl.ds(h * size, size)
+
+    def spread_copy(phase, b, h, target, way):
+        part = (image, fresh)[phase].at[b, rows_of(h)]
+        return remote(
+            part, part, ag_send.at[phase, b, h, way], ag_recv.at[phase, b, h], (row, target)
+        )
+
+    def spread_start(phase, h):
+        launch(spread_copy(phase, col, h, lax.rem(col + 1, col_total), 0), col < last)
+        launch(spread_copy(phase, col, h, lax.rem(col + last, col_total), 1), col > 0)
+
+    def onward(b):
+        return jnp.where(b < col, lax.rem(col + 1, col_total), lax.rem(col + last, col_total))
+
+    def more(b):
+        return jnp.where(b < col, col < last, col > 0)
+
+    def spread_step(phase, b, h):
+        copy = spread_copy(phase, b, h, onward(b), 0)
+        copy.wait_recv()
+        launch(copy, more(b))
+
+    def code_copy(b, target, way):
+        return remote(
+            codes.at[b], codes.at[b], code_send.at[b, way], code_recv.at[b], (row, target)
+        )
+
+    def sum_copy(phase, b, h):
+        side = jnp.where(b > col, 0, 1)
+        target = jnp.where(b > col, lax.rem(col + 1, col_total), lax.rem(col + last, col_total))
+        return remote(
+            stage.at[b, rows_of(h)],
+            slots.at[side, b, rows_of(h)],
+            rs_send.at[phase, b, h],
+            rs_recv.at[phase, side, b, h],
+            (row, target),
+        )
+
+    def fed(b):
+        return jnp.where(b > col, col > 0, col < last)
+
+    sums = []
+
+    def sum_edge(phase, b, h):
+        launch(sum_copy(phase, b, h), jnp.logical_not(fed(b)), sums)
+
+    def sum_step(phase, b, h):
+        copy = sum_copy(phase, b, h)
+
+        @pl.when(fed(b))
+        def _():
+            side = jnp.where(b > col, 0, 1)
+            copy.wait_recv()
+            held = stage[b, rows_of(h)].astype(f32) + slots[side, b, rows_of(h)].astype(f32)
+            stage[b, rows_of(h)] = held.astype(stage.dtype)
+
+        launch(copy, fed(b), sums)
+
+    def sum_own(phase, h):
+        for side, condition in ((0, col > 0), (1, col < last)):
+
+            @pl.when(condition)
+            def _():
+                slot = slots.at[side, col, rows_of(h)]
+                remote(
+                    slot, slot, rs_send.at[phase, col, h], rs_recv.at[phase, side, col, h], (row, onward(col))
+                ).wait_recv()
+                own_sum[rows_of(h)] += slots[side, col, rows_of(h)].astype(f32)
+
+    def norm_rows(source, gain, target, index, h):
+        for start in range(h * size, (h + 1) * size, 32):
+            rows = pl.ds(start, 32)
+            target[index, rows] = layer_norm(source[rows], gain[...]).astype(target.dtype)
+
+    def columns(width, tile, body):
+        def step(j, carry):
+            body(pl.ds(pl.multiple_of(j * tile, tile), tile))
+            return carry
+
+        lax.fori_loop(0, width // tile, step, 0)
+
+    loads[0].wait()
+    norm_rows(tokens, gain_one, image, col, 0)
+
+    named = jnp.broadcast_to(ids_in[...], (tok, tok)).astype(f32)
+    across_ids = named.T
+    earlier = lax.broadcasted_iota(jnp.int32, (tok, tok), 0) < lax.broadcasted_iota(
+        jnp.int32, (tok, tok), 1
+    )
+    rank = jnp.sum(jnp.where(earlier & (named == across_ids), 1.0, 0.0), axis=0, keepdims=True)
+    code = across_ids[0:8] * capacity + rank
+    codes[col] = code.astype(jnp.int32)
+
+    pl.semaphore_wait(barrier, row_total + col_total - 2)
+    spread_start(0, 0)
+    gather_start(0)
+    for h in range(1, parts):
+        norm_rows(tokens, gain_one, image, col, h)
+        spread_start(0, h)
+    launch(code_copy(col, lax.rem(col + 1, col_total), 0), col < last)
+    launch(code_copy(col, lax.rem(col + last, col_total), 1), col > 0)
+    gather_start(1)
+
+    def project(b):
+        def tile(at):
+            inner = matmul(image[b], qkv[:, at])
+            proj[pl.ds(pl.multiple_of(b * tok, tok), tok), at] = inner.astype(proj.dtype)
+
+        columns(qkv.shape[1], 512, tile)
+
+    def arrive(phase, k):
+        for h in range(parts):
+            spread_step(phase, near[k], h)
+
+    def arrive_code(k):
+        copy = code_copy(near[k], onward(near[k]), 0)
+        copy.wait_recv()
+        launch(copy, more(near[k]))
+
+    arrive(0, 1)
+    arrive_code(1)
+    gather_relay(0)
+    for k in range(2, col_total - 1):
+        arrive(0, k)
+        arrive_code(k)
+    gather_relay(1)
+    gather_start(2)
+    gather_start(3)
+    gather_finish(0)
+    gather_finish(1)
+    gather_complete(0)
+    for k in range(col_total - 1):
+        project(near[k])
+    arrive(0, last)
+    arrive_code(last)
+    project(near[last])
+    gather_complete(1)
+
+    def attend(b):
+        mine = pl.ds(pl.multiple_of(b * tok, tok), tok)
+        for n in range(heads):
+            base = 3 * n * head_dim
+            query = proj[mine, base : base + head_dim]
+            keys = proj[:, base + head_dim : base + 2 * head_dim]
+            values = proj[:, base + 2 * head_dim : base + 3 * head_dim]
+            scores = lax.dot_general(
+                query, keys, (((1,), (1,)), ((), ())), preferred_element_type=f32
+            )
+            scores = scores * (head_dim ** (-0.5))
+            weights = jnp.exp(scores - jnp.max(scores, axis=-1, keepdims=True))
+            weights = weights / jnp.sum(weights, axis=-1, keepdims=True)
+            attended[:, n * head_dim : (n + 1) * head_dim] = matmul(
+                weights.astype(jnp.bfloat16), values
+            ).astype(jnp.bfloat16)
+
+    def head_terms(b, store):
+        def tile(at):
+            store(at, matmul(attended[...], outw[:, at]))
+
+        columns(model, 512, tile)
+
+    def to_stage(b):
+        def store(at, inner):
+            stage[b, :, at] = inner.astype(stage.dtype)
+
+        return store
+
+    def to_own(at, inner):
+        own_sum[:, at] = inner
+
+    for k in range(last):
+        attend(far[k])
+        head_terms(far[k], to_stage(far[k]))
+        sum_edge(0, far[k], 0)
+    for h in range(1, parts):
+        for k in range(last):
+            sum_edge(0, far[k], h)
+    attend(col)
+    head_terms(col, to_own)
+
+    def placing(b):
+        slot = lax.broadcasted_iota(jnp.int32, (row_total * capacity, tok), 0)
+        wanted = slot + lax.div(col, 2) * capacity
+        for n in range(1, row_total):
+            wanted += jnp.where(slot >= n * capacity, (col_total // 2 - 1) * capacity, 0)
+        return jnp.where(wanted == codes[b][0:1], 1.0, 0.0)
+
+    def group(index):
+        return pl.ds(pl.multiple_of(index * capacity, capacity), capacity)
+
+    def out_copy(b, source, target):
+        return remote(
+            table.at[b, group(target)],
+            landed.at[b, group(source)],
+            out_send.at[b, target],
+            out_recv.at[b, source],
+            (target, col),
+        )
+
+    def back_copy(b, holder, target):
+        return remote(
+            landed.at[b, group(target)],
+            returned.at[b, group(holder)],
+            back_send.at[b, target],
+            back_recv.at[b, holder],
+            (target, col),
+        )
+
+    def dispatch(b):
+        place = placing(b).astype(jnp.bfloat16)
+
+        def tile(at):
+            table[b, :, at] = matmul(place, fresh[b, :, at]).astype(table.dtype)
+
+        columns(model, 512, tile)
+        for flip in (2, 4, 6, 3, 5, 7, 1):
+            launch(out_copy(b, row, lax.bitwise_xor(row, flip)))
+        landed[b, group(row)] = table[b, group(row)]
+
+    def with_gelu(inner):
+        return (inner * (1.0 + lax.erf(inner * (0.5**0.5))) * 0.5).astype(jnp.bfloat16)
+
+    def expert(b):
+        for flip in range(1, row_total):
+            other = lax.bitwise_xor(row, flip)
+            out_copy(b, other, row).wait_recv()
+
+        def up(at):
+            units[:, at] = with_gelu(matmul(landed[b], first[:, at]))
+
+        columns(first.shape[1], 512, up)
+
+        def down(at):
+            landed[b, :, at] = matmul(units[...], second[:, at]).astype(landed.dtype)
+
+        columns(model, 512, down)
+        for flip in (2, 4, 6, 3, 5, 7, 1):
+            launch(back_copy(b, row, lax.bitwise_xor(row, flip)))
+        returned[b, group(row)] = landed[b, group(row)]
+
+    def dense(b, store):
+        def up(at):
+            units[:, at] = with_gelu(matmul(fresh[b], upw[:, at]))
+
+        columns(upw.shape[1], 512, up)
+
+        def down(at):
+            store(at, matmul(units[...], downw[:, at]))
+
+        columns(model, 512, down)
+
+    def combine(b, own):
+        for flip in range(1, row_total):
+            other = lax.bitwise_xor(row, flip)
+            back_copy(b, other, row).wait_recv()
+        pick = placing(b).T.astype(jnp.bfloat16)
+
+        def tile(at):
+            inner = matmul(pick, returned[b, :, at])
+            if own:
+                own_sum[:, at] += inner
+            else:
+                stage[b, :, at] = (stage[b, :, at].astype(f32) + inner).astype(stage.dtype)
+
+        columns(model, 512, tile)
+
+    def close_hidden(h):
+        sum_own(0, h)
+        rows = rows_of(h)
+        hidden[rows] = (tokens[rows].astype(f32) + own_sum[rows]).astype(hidden.dtype)
+        norm_rows(hidden, gain_two, fresh, col, h)
+        spread_start(1, h)
+
+    for k in range(last):
+        sum_step(0, far[k], 0)
+    close_hidden(0)
+    gather_relay(2)
+    for h in range(1, parts):
+        for k in range(last):
+            sum_step(0, far[k], h)
+            spread_step(1, near[k + 1], h - 1)
+        close_hidden(h)
+        if h == 1:
+            gather_relay(3)
+    gather_finish(2)
+    dispatch(col)
+    for k in range(1, col_total):
+        spread_step(1, near[k], parts - 1)
+        dispatch(near[k])
+        if k == 1:
+            gather_finish(3)
+    drain(sums)
+    loads[5].wait()
+    loads[6].wait()
+    expert(near[0])
+    gather_complete(2)
+    gather_complete(3)
+    for k in range(1, col_total):
+        expert(near[k])
+        dense(near[k], to_stage(near[k]))
+    dense(col, to_own)
+    for k in range(1, col_total):
+        combine(near[k], False)
+        for h in range(parts):
+            sum_edge(1, near[k], h)
+    combine(col, True)
+    for h in range(parts):
+        for k in range(last):
+            sum_step(1, far[k], h)
+    for h in range(parts):
+        sum_own(1, h)
+        rows = rows_of(h)
+        result[rows] = (hidden[rows].astype(f32) + own_sum[rows]).astype(result.dtype)
+    drain(sums)
+    drain(finish)
+
+
+def fused_block(tokens, gain_one, qkv_part, out_part, gain_two, up_part, down_part, ids, first, second, capacity, heads):
+    row_total = lax.axis_size("row")
+    col_total = lax.axis_size("col")
+    tok, model = tokens.shape
+    parts = 2
+    hbm, vmem = pl.BlockSpec(memory_space=pl.ANY), pl.BlockSpec(memory_space=pltpu.VMEM)
+    bf16 = jnp.bfloat16
+    three = qkv_part.shape[1]
+    width = out_part.shape[0]
+    slot_count = row_total * capacity
+    dma = pltpu.SemaphoreType.DMA
+    scratch = [
+        pltpu.VMEM((tok, model), bf16),
+        pltpu.VMEM((col_total, tok, model), bf16),
+        pltpu.VMEM((col_total, tok, model), bf16),
+        pltpu.VMEM((row_total * qkv_part.shape[0], three), bf16),
+        pltpu.VMEM((width, row_total * out_part.shape[1]), bf16),
+        pltpu.VMEM((row_total * up_part.shape[0], up_part.shape[1]), bf16),
+        pltpu.VMEM((down_part.shape[0], row_total * down_part.shape[1]), bf16),
+        pltpu.VMEM(first.shape, bf16),
+        pltpu.VMEM(second.shape, bf16),
+        pltpu.VMEM((col_total * tok, three), bf16),
+        pltpu.VMEM((tok, width), bf16),
+        pltpu.VMEM((col_total, tok, model), bf16),
+        pltpu.VMEM((2, col_total, tok, model), bf16),
+        pltpu.VMEM((tok, model), jnp.float32),
+        pltpu.VMEM((tok, model), bf16),
+        pltpu.VMEM((col_total, slot_count, model), bf16),
+        pltpu.VMEM((col_total, slot_count, model), bf16),
+        pltpu.VMEM((col_total, slot_count, model), bf16),
+        pltpu.VMEM((tok, max(up_part.shape[1], first.shape[1])), bf16),
+        pltpu.VMEM((col_total, 8, tok), jnp.int32),
+        dma((7,)),
+        dma((2, col_total, parts, 2)),
+        dma((2, col_total, parts)),
+        dma((col_total, 2)),
+        dma((col_total,)),
+        dma((2, col_total, parts)),
+        dma((2, 2, col_total, parts)),
+        dma((4, 9)),
+        dma((4, 9)),
+        dma((col_total, row_total)),
+        dma((col_total, row_total)),
+        dma((col_total, row_total)),
+        dma((col_total, row_total)),
+    ]
+    return pl.pallas_call(
+        functools.partial(block_body, (row_total, col_total, capacity, heads, parts)),
+        out_shape=jax.ShapeDtypeStruct((tok, model), bf16),
+        in_specs=[hbm, vmem, vmem, vmem] + [hbm] * 6,
+        out_specs=vmem,
+        scratch_shapes=scratch,
+        compiler_params=pltpu.CompilerParams(
+            collective_id=0, has_side_effects=True, vmem_limit_bytes=67043328
+        ),
+        name="block",
+    )(
+        tokens,
+        gain_one.reshape(1, model),
+        gain_two.reshape(1, model),
+        ids,
+        qkv_part,
+        out_part,
+        up_part,
+        down_part,
+        first,
+        second,
+    )
+
+
 def shards(
     tokens,
     ln1_gain,
@@ -399,6 +909,21 @@
     capacity = max(2, 2 * tok_count // expert_count)
     head_count, head_dim = qkv_weight.shape[1], qkv_weight.shape[3]
     seq_len = tok_count * col_total
+    if row_total == 8 and col_total % 2 == 0 and capacity % 16 == 0:
+        return fused_block(
+            tokens,
+            ln1_gain,
+            qkv_weight.reshape(qkv_weight.shape[0], -1),
+            out_weight,
+            ln2_gain,
+            ffn_in,
+            ffn_out,
+            expert_ids,
+            expert_in[0],
+            expert_out[0],
+            capacity,
+            head_count,
+        )
 
     ids_block = jnp.broadcast_to(expert_ids[:, 0][None, :], (8, tok_count))
     qkv_whole, out_whole, image_rows, ids_all = exchange(

time: 263 us -> 242 us (0.920)
  matrix products: 20.5 us -> 0 us
  Pallas kernels: 223 us -> 236 us
  local copies, waits for them, and re-layouts: 12 us -> 5.95 us
  other arithmetic: 4.63 us -> 0 us
    dot_general x7 -> x0, matrix products: 20.5 us -> none  [the longest x5 13.3 us: matmul(): return jnp.dot(a, b, preferred_element_type=jnp.float32)]
    pallas_call x7 -> x1, Pallas kernels: 223 us -> 236 us  [fused_block(): pl.pallas_call(functools.partial(block_body, (row_total, col_total, capac...]
    unnamed x29 -> x3, local copies, waits for them, and re-layouts: 8.44 us -> 4.8 us
where the time goes in v1:
time: 242 us
  Pallas kernels  236 us (98%)
  local copies, waits for them, and re-layouts  5.95 us (2%)
    pallas_call x1, Pallas kernels, fused_block(): pl.pallas_call(functools.partial(block_body, (row_total, col_total, capac...  236 us

profile of v1, /device:TPU:6, one launch (start us, length us, event | category | flops | bytes accessed | tf_op | source)
XLA Modules:
  0.0 242.0 jit_solution(4761917626230018226)
XLA Ops:
  0.0 1.5 copy.13
  1.5 1.2 copy.15.refs_4_
  2.7 1.4 copy.14.refs_3_
  4.1 236.0 %block.1 = bf16[128,2048]{1,0:T(8,128)(2,1)} custom-call(bf16[128,2048]{1,0:T(8,128)(2,1)} %refs_0_.1, f32[1,2048]{1,0:T(1,128)} %bitcast.8, f32[1,2048]{1,0:T(1,128)} %bitcast.9, s32[128,1]{1,0:T(8,128)} %copy.14.refs_3_, bf16[256,1536]{1,0:T(8,128)(2,1)} %copy.15.refs_4_, bf16[512,256]{1,0:T(8,128)(2,1)} %refs_5_.1, bf16[256,2048]{1,0:T(8,128)(2,1)} %refs_6_.1, ...), custom_call_target="tpu_custom_call" | custom-call | tf_op jit(solution)/shard_map/block/pallas_call | solution.py:867
  240.1 1.9 copy.17

commit v2 on v1

--- a/solution.py
+++ b/solution.py
@@ -390,7 +390,22 @@
 
 
 def far_first(total):
-    return [sorted(range(total), key=lambda b: (-abs(b - c), -b)) for c in range(total)]
+    last = total - 1
+    return [
+        sorted(range(total), key=lambda b: (-abs(b - c), c if b > c else last - c))
+        for c in range(total)
+    ]
+
+
+def late_last(total):
+    last = total - 1
+    return [
+        sorted(
+            [b for b in range(total) if b != c],
+            key=lambda b: b + c if b > c else 2 * last - b - c,
+        )
+        for c in range(total)
+    ]
 
 
 def block_body(sizes, *refs):
@@ -398,9 +413,9 @@
     (tokens_in, gain_one, gain_two, ids_in, qkv_in, out_in, up_in, down_in, first_in, second_in) = refs[:10]
     result = refs[10]
     (tokens, image, fresh, qkv, outw, upw, downw, first, second, proj, attended, stage, slots) = refs[11:24]
-    (own_sum, hidden, table, landed, returned, units, codes) = refs[24:31]
-    (load_sem, ag_send, ag_recv, code_send, code_recv, rs_send, rs_recv) = refs[31:38]
-    (gather_send, gather_recv, out_send, out_recv, back_send, back_recv) = refs[38:]
+    (own_sum, hidden, table, landed, returned, units, inner_units, codes) = refs[24:32]
+    (load_sem, ag_send, ag_recv, code_send, code_recv, rs_send, rs_recv) = refs[32:39]
+    (gather_send, gather_recv, out_send, out_recv, back_send, back_recv) = refs[39:]
     row = lax.axis_index("row")
     col = lax.axis_index("col")
     last = col_total - 1
@@ -441,21 +456,31 @@
                 pl.when(condition)(copy.wait_send)
         items.clear()
 
-    wholes = [(qkv, qkv_in, 0), (outw, out_in, 1), (upw, up_in, 0), (downw, down_in, 1)]
+    cut = qkv_in.shape[0] // 2
+    wholes = [
+        (qkv, qkv_in, 0, 0, cut),
+        (qkv, qkv_in, 0, cut, cut),
+        (outw, out_in, 1, 0, out_in.shape[0]),
+        (upw, up_in, 0, 0, up_in.shape[0]),
+        (downw, down_in, 1, 0, down_in.shape[0] // 2),
+        (downw, down_in, 1, down_in.shape[0] // 2, down_in.shape[0] // 2),
+    ]
 
     def piece(g, index, half=None):
-        whole, part, axis = wholes[g]
+        whole, part, axis, start, count = wholes[g]
         depth, width = part.shape
-        start, count = (0, depth) if half is None else (half * (depth // 2), depth // 2)
+        if half is not None:
+            start, count = start + half * (count // 2), count // 2
         if axis == 0:
             return whole.at[pl.ds(pl.multiple_of(index * depth + start, count), count)]
         return whole.at[pl.ds(start, count), pl.ds(pl.multiple_of(index * width, width), width)]
 
     loads = [pltpu.make_async_copy(tokens_in, tokens, load_sem.at[0])]
-    for g in range(4):
-        loads.append(pltpu.make_async_copy(wholes[g][1], piece(g, row), load_sem.at[1 + g]))
-    loads.append(pltpu.make_async_copy(first_in, first, load_sem.at[5]))
-    loads.append(pltpu.make_async_copy(second_in, second, load_sem.at[6]))
+    for g, (_, part, _, start, count) in enumerate(wholes):
+        source = part.at[pl.ds(start, count)]
+        loads.append(pltpu.make_async_copy(source, piece(g, row), load_sem.at[1 + g]))
+    loads.append(pltpu.make_async_copy(first_in, first, load_sem.at[7]))
+    loads.append(pltpu.make_async_copy(second_in, second, load_sem.at[8]))
     for load in loads:
         load.start()
 
@@ -497,6 +522,7 @@
         gather_wait(g, 8, flipped(across, 1), 1)
 
     near = [chosen([order[k] for order in near_first(col_total)], col) for k in range(col_total)]
+    late = [chosen([order[k] for order in late_last(col_total)], col) for k in range(last)]
     far = [chosen([order[k] for order in far_first(col_total)], col) for k in range(col_total)]
 
     def rows_of(h):
@@ -518,10 +544,13 @@
     def more(b):
         return jnp.where(b < col, col < last, col > 0)
 
-    def spread_step(phase, b, h):
-        copy = spread_copy(phase, b, h, onward(b), 0)
-        copy.wait_recv()
-        launch(copy, more(b))
+    def spread_at(phase, distance, h):
+        for other in (col - distance, col + distance):
+            valid = (other >= 0) & (other <= last)
+            b = lax.rem(other + col_total, col_total)
+            copy = spread_copy(phase, b, h, onward(b), 0)
+            pl.when(valid)(copy.wait_recv)
+            launch(copy, valid & more(b))
 
     def code_copy(b, target, way):
         return remote(
@@ -571,8 +600,9 @@
                 own_sum[rows_of(h)] += slots[side, col, rows_of(h)].astype(f32)
 
     def norm_rows(source, gain, target, index, h):
-        for start in range(h * size, (h + 1) * size, 32):
-            rows = pl.ds(start, 32)
+        step = min(size, 32)
+        for start in range(h * size, (h + 1) * size, step):
+            rows = pl.ds(start, step)
             target[index, rows] = layer_norm(source[rows], gain[...]).astype(target.dtype)
 
     def columns(width, tile, body):
@@ -580,13 +610,13 @@
             body(pl.ds(pl.multiple_of(j * tile, tile), tile))
             return carry
 
-        lax.fori_loop(0, width // tile, step, 0)
+        lax.fori_loop(0, width // tile, step, 0, unroll=True)
 
     loads[0].wait()
     norm_rows(tokens, gain_one, image, col, 0)
 
-    named = jnp.broadcast_to(ids_in[...], (tok, tok)).astype(f32)
-    across_ids = named.T
+    across_ids = jnp.broadcast_to(ids_in[...], (tok, tok)).astype(f32)
+    named = across_ids.T
     earlier = lax.broadcasted_iota(jnp.int32, (tok, tok), 0) < lax.broadcasted_iota(
         jnp.int32, (tok, tok), 1
     )
@@ -597,12 +627,12 @@
     pl.semaphore_wait(barrier, row_total + col_total - 2)
     spread_start(0, 0)
     gather_start(0)
+    gather_start(1)
     for h in range(1, parts):
         norm_rows(tokens, gain_one, image, col, h)
         spread_start(0, h)
     launch(code_copy(col, lax.rem(col + 1, col_total), 0), col < last)
     launch(code_copy(col, lax.rem(col + last, col_total), 1), col > 0)
-    gather_start(1)
 
     def project(b):
         def tile(at):
@@ -611,41 +641,45 @@
 
         columns(qkv.shape[1], 512, tile)
 
-    def arrive(phase, k):
+    def arrive(distance):
         for h in range(parts):
-            spread_step(phase, near[k], h)
-
-    def arrive_code(k):
-        copy = code_copy(near[k], onward(near[k]), 0)
-        copy.wait_recv()
-        launch(copy, more(near[k]))
-
-    arrive(0, 1)
-    arrive_code(1)
+            spread_at(0, distance, h)
+        for other in (col - distance, col + distance):
+            valid = (other >= 0) & (other <= last)
+            b = lax.rem(other + col_total, col_total)
+            copy = code_copy(b, onward(b), 0)
+            pl.when(valid)(copy.wait_recv)
+            launch(copy, valid & more(b))
+
+    for distance in range(1, max(2, last - 1)):
+        arrive(distance)
     gather_relay(0)
-    for k in range(2, col_total - 1):
-        arrive(0, k)
-        arrive_code(k)
     gather_relay(1)
     gather_start(2)
-    gather_start(3)
+    for distance in range(max(2, last - 1), last):
+        arrive(distance)
     gather_finish(0)
     gather_finish(1)
     gather_complete(0)
-    for k in range(col_total - 1):
+    gather_complete(1)
+    for k in range(last):
         project(near[k])
-    arrive(0, last)
-    arrive_code(last)
+    gather_relay(2)
+    gather_start(3)
+    gather_start(4)
+    gather_start(5)
+    if last > 1:
+        arrive(last)
     project(near[last])
-    gather_complete(1)
+    gather_finish(2)
 
     def attend(b):
         mine = pl.ds(pl.multiple_of(b * tok, tok), tok)
         for n in range(heads):
-            base = 3 * n * head_dim
+            base, jump = n * head_dim, heads * head_dim
             query = proj[mine, base : base + head_dim]
-            keys = proj[:, base + head_dim : base + 2 * head_dim]
-            values = proj[:, base + 2 * head_dim : base + 3 * head_dim]
+            keys = proj[:, base + jump : base + jump + head_dim]
+            values = proj[:, base + 2 * jump : base + 2 * jump + head_dim]
             scores = lax.dot_general(
                 query, keys, (((1,), (1,)), ((), ())), preferred_element_type=f32
             )
@@ -673,13 +707,12 @@
 
     for k in range(last):
         attend(far[k])
+        if k == 0:
+            gather_complete(2)
         head_terms(far[k], to_stage(far[k]))
         sum_edge(0, far[k], 0)
-    for h in range(1, parts):
-        for k in range(last):
-            sum_edge(0, far[k], h)
-    attend(col)
-    head_terms(col, to_own)
+    for k in range(last):
+        sum_edge(0, far[k], 1)
 
     def placing(b):
         slot = lax.broadcasted_iota(jnp.int32, (row_total * capacity, tok), 0)
@@ -741,16 +774,21 @@
             launch(back_copy(b, row, lax.bitwise_xor(row, flip)))
         returned[b, group(row)] = landed[b, group(row)]
 
+    def dense_up(b):
+        def up(at):
+            inner_units[:, at] = with_gelu(matmul(fresh[b], upw[:, at]))
+
+        columns(upw.shape[1], 512, up)
+
+    def dense_down(store):
+        def down(at):
+            store(at, matmul(inner_units[...], downw[:, at]))
+
+        columns(model, 512, down)
+
     def dense(b, store):
-        def up(at):
-            units[:, at] = with_gelu(matmul(fresh[b], upw[:, at]))
-
-        columns(upw.shape[1], 512, up)
-
-        def down(at):
-            store(at, matmul(units[...], downw[:, at]))
-
-        columns(model, 512, down)
+        dense_up(b)
+        dense_down(store)
 
     def combine(b, own):
         for flip in range(1, row_total):
@@ -776,40 +814,79 @@
 
     for k in range(last):
         sum_step(0, far[k], 0)
-    close_hidden(0)
-    gather_relay(2)
-    for h in range(1, parts):
-        for k in range(last):
-            sum_step(0, far[k], h)
-            spread_step(1, near[k + 1], h - 1)
+    attend(col)
+    head_terms(col, to_own)
+    def even_hops(h):
+        for distance in range(2, last + 1, 2):
+            if 0 <= h - distance // 2 - 1 < parts:
+                spread_at(1, distance, h - distance // 2 - 1)
+
+    def odd_hops(h, first_hop):
+        for distance in range(1 if first_hop else 3, 2 if first_hop else last + 1, 2):
+            if 0 <= h - (distance + 1) // 2 < parts:
+                spread_at(1, distance, h - (distance + 1) // 2)
+
+    def send_on(b):
+        combine(b, False)
+        for h in range(parts):
+            sum_edge(1, b, h)
+
+    for h in range(parts):
+        if h > 0:
+            for k in range(last):
+                sum_step(0, far[k], h)
+        even_hops(h)
         close_hidden(h)
-        if h == 1:
+        if h + 2 < parts:
+            for k in range(last):
+                sum_edge(0, far[k], h + 2)
+        odd_hops(h, True)
+        odd_hops(h, False)
+        if h == parts // 4:
             gather_relay(3)
-    gather_finish(2)
+        if h == parts - 2:
+            gather_relay(4)
+    even_hops(parts)
+    odd_hops(parts, True)
+    dispatch(near[1])
+    gather_relay(5)
+    odd_hops(parts, False)
+    gather_finish(3)
+    even_hops(parts + 1)
+    dispatch(near[2])
+    odd_hops(parts + 1, False)
+    drain(sums)
+    loads[7].wait()
+    loads[8].wait()
+    gather_finish(4)
+    expert(near[1])
+    dispatch(near[3])
+    gather_complete(3)
+    dense_up(near[1])
+    gather_finish(5)
+    gather_complete(4)
+    gather_complete(5)
+    dense_down(to_stage(near[1]))
+    expert(near[2])
     dispatch(col)
-    for k in range(1, col_total):
-        spread_step(1, near[k], parts - 1)
-        dispatch(near[k])
-        if k == 1:
-            gather_finish(3)
-    drain(sums)
-    loads[5].wait()
-    loads[6].wait()
-    expert(near[0])
-    gather_complete(2)
-    gather_complete(3)
-    for k in range(1, col_total):
-        expert(near[k])
-        dense(near[k], to_stage(near[k]))
+    send_on(near[1])
+    dense(near[2], to_stage(near[2]))
+    expert(near[3])
+    send_on(near[2])
+    dense(near[3], to_stage(near[3]))
+    sum_step(1, late[0], 0)
+    expert(col)
+    for h in range(1, parts - 1):
+        sum_step(1, late[0], h)
+    send_on(near[3])
+    sum_step(1, late[0], parts - 1)
     dense(col, to_own)
-    for k in range(1, col_total):
-        combine(near[k], False)
-        for h in range(parts):
-            sum_edge(1, near[k], h)
+    sum_step(1, late[1], 0)
     combine(col, True)
-    for h in range(parts):
-        for k in range(last):
-            sum_step(1, far[k], h)
+    for h in range(1, parts + 1):
+        if h < parts:
+            sum_step(1, late[1], h)
+        sum_step(1, late[2], h - 1)
     for h in range(parts):
         sum_own(1, h)
         rows = rows_of(h)
@@ -822,7 +899,7 @@
     row_total = lax.axis_size("row")
     col_total = lax.axis_size("col")
     tok, model = tokens.shape
-    parts = 2
+    parts = 4
     hbm, vmem = pl.BlockSpec(memory_space=pl.ANY), pl.BlockSpec(memory_space=pltpu.VMEM)
     bf16 = jnp.bfloat16
     three = qkv_part.shape[1]
@@ -848,17 +925,18 @@
         pltpu.VMEM((col_total, slot_count, model), bf16),
         pltpu.VMEM((col_total, slot_count, model), bf16),
         pltpu.VMEM((col_total, slot_count, model), bf16),
-        pltpu.VMEM((tok, max(up_part.shape[1], first.shape[1])), bf16),
+        pltpu.VMEM((tok, first.shape[1]), bf16),
+        pltpu.VMEM((tok, up_part.shape[1]), bf16),
         pltpu.VMEM((col_total, 8, tok), jnp.int32),
-        dma((7,)),
+        dma((9,)),
         dma((2, col_total, parts, 2)),
         dma((2, col_total, parts)),
         dma((col_total, 2)),
         dma((col_total,)),
         dma((2, col_total, parts)),
         dma((2, 2, col_total, parts)),
-        dma((4, 9)),
-        dma((4, 9)),
+        dma((6, 9)),
+        dma((6, 9)),
         dma((col_total, row_total)),
         dma((col_total, row_total)),
         dma((col_total, row_total)),
@@ -871,7 +949,7 @@
         out_specs=vmem,
         scratch_shapes=scratch,
         compiler_params=pltpu.CompilerParams(
-            collective_id=0, has_side_effects=True, vmem_limit_bytes=67043328
+            collective_id=0, has_side_effects=True, vmem_limit_bytes=62 * 2**20
         ),
         name="block",
     )(
@@ -909,16 +987,16 @@
     capacity = max(2, 2 * tok_count // expert_count)
     head_count, head_dim = qkv_weight.shape[1], qkv_weight.shape[3]
     seq_len = tok_count * col_total
-    if row_total == 8 and col_total % 2 == 0 and capacity % 16 == 0:
+    if row_total == 8 and col_total == 4 and capacity % 16 == 0:
         return fused_block(
             tokens,
             ln1_gain,
-            qkv_weight.reshape(qkv_weight.shape[0], -1),
+            jnp.swapaxes(qkv_weight, 1, 2).reshape(qkv_weight.shape[0], -1),
             out_weight,
             ln2_gain,
             ffn_in,
             ffn_out,
-            expert_ids,
+            expert_ids.reshape(1, tok_count),
             expert_in[0],
             expert_out[0],
             capacity,

time: 242 us -> 183 us (0.76)
  Pallas kernels: 236 us -> 176 us
    pallas_call x1, Pallas kernels: 236 us -> 176 us  [fused_block(): pl.pallas_call(functools.partial(block_body, (row_total, col_total, capac...]
    unnamed x3 -> x1, local copies, waits for them, and re-layouts: 4.8 us -> 1.88 us
where the time goes in v2:
time: 183 us; the launch traced here: 181 us
  Pallas kernels  176 us (96%)
  local copies, waits for them, and re-layouts  4.23 us (2%)
    pallas_call x1, Pallas kernels, fused_block(): pl.pallas_call(functools.partial(block_body, (row_total, col_total, capac...  176 us

profile of v2, /device:TPU:6, one launch (start us, length us, event | category | flops | bytes accessed | tf_op | source)
XLA Modules:
  0.0 180.6 jit_solution(11981585653681324967)
XLA Ops:
  0.0 2.3 %reshape.15.refs_4_ = bf16[256,1536]{1,0:T(8,128)(2,1)} reshape(bf16[256,3,4,128]{3,2,1,0:T(4,128)(2,1)} %bitcast.8) | data formatting | bytes 1572864 | tf_op jit(solution)/shard_map/reshape | solution.py:994
  2.3 176.3 %block.1 = bf16[128,2048]{1,0:T(8,128)(2,1)} custom-call(bf16[128,2048]{1,0:T(8,128)(2,1)} %refs_0_.1, f32[1,2048]{1,0:T(1,128)} %bitcast.9, f32[1,2048]{1,0:T(1,128)} %bitcast.10, s32[1,128]{1,0:T(1,128)} %bitcast.11, bf16[256,1536]{1,0:T(8,128)(2,1)} %reshape.15.refs_4_, bf16[512,256]{1,0:T(8,128)(2,1)} %refs_5_.1, bf16[256,2048]{1,0:T(8,128)(2,1)} %refs_6_.1, ...), custom_call_target="tpu_custom_call" | custom-call | tf_op jit(solution)/shard_map/block/pallas_call | solution.py:945
  178.7 1.9 %copy.12 = bf16[128,2048]{1,0:T(8,128)(2,1)} copy(bf16[128,2048]{1,0:T(8,128)(2,1)} %block.1) | data formatting | bytes 1048576

commit v3 on v2

--- a/solution.py
+++ b/solution.py
@@ -397,25 +397,15 @@
     ]
 
 
-def late_last(total):
-    last = total - 1
-    return [
-        sorted(
-            [b for b in range(total) if b != c],
-            key=lambda b: b + c if b > c else 2 * last - b - c,
-        )
-        for c in range(total)
-    ]
-
-
 def block_body(sizes, *refs):
     row_total, col_total, capacity, heads, parts = sizes
-    (tokens_in, gain_one, gain_two, ids_in, qkv_in, out_in, up_in, down_in, first_in, second_in) = refs[:10]
-    result = refs[10]
+    (tokens_in, gain_one_in, gain_two_in, ids_in, qkv_in, out_in, up_in, down_in, first_in, second_in) = refs[:10]
+    result_out = refs[10]
     (tokens, image, fresh, qkv, outw, upw, downw, first, second, proj, attended, stage, slots) = refs[11:24]
     (own_sum, hidden, table, landed, returned, units, inner_units, codes) = refs[24:32]
     (load_sem, ag_send, ag_recv, code_send, code_recv, rs_send, rs_recv) = refs[32:39]
-    (gather_send, gather_recv, out_send, out_recv, back_send, back_recv) = refs[39:]
+    (gather_send, gather_recv, out_send, out_recv, back_send, back_recv) = refs[39:45]
+    (gain_one, gain_two, ids, result, store_sem) = refs[45:]
     row = lax.axis_index("row")
     col = lax.axis_index("col")
     last = col_total - 1
@@ -481,7 +471,12 @@
         loads.append(pltpu.make_async_copy(source, piece(g, row), load_sem.at[1 + g]))
     loads.append(pltpu.make_async_copy(first_in, first, load_sem.at[7]))
     loads.append(pltpu.make_async_copy(second_in, second, load_sem.at[8]))
-    for load in loads:
+    small = [
+        pltpu.make_async_copy(gain_one_in, gain_one, load_sem.at[9]),
+        pltpu.make_async_copy(ids_in, ids, load_sem.at[10]),
+        pltpu.make_async_copy(gain_two_in, gain_two, load_sem.at[11]),
+    ]
+    for load in loads[:1] + small + loads[1:]:
         load.start()
 
     partner, by_x, by_y = flipped(row, 1), flipped(row, 2), flipped(row, 4)
@@ -522,7 +517,6 @@
         gather_wait(g, 8, flipped(across, 1), 1)
 
     near = [chosen([order[k] for order in near_first(col_total)], col) for k in range(col_total)]
-    late = [chosen([order[k] for order in late_last(col_total)], col) for k in range(last)]
     far = [chosen([order[k] for order in far_first(col_total)], col) for k in range(col_total)]
 
     def rows_of(h):
@@ -613,9 +607,11 @@
         lax.fori_loop(0, width // tile, step, 0, unroll=True)
 
     loads[0].wait()
+    for load in small:
+        load.wait()
     norm_rows(tokens, gain_one, image, col, 0)
 
-    across_ids = jnp.broadcast_to(ids_in[...], (tok, tok)).astype(f32)
+    across_ids = jnp.broadcast_to(ids[...], (tok, tok)).astype(f32)
     named = across_ids.T
     earlier = lax.broadcasted_iota(jnp.int32, (tok, tok), 0) < lax.broadcasted_iota(
         jnp.int32, (tok, tok), 1
@@ -846,53 +842,59 @@
             gather_relay(3)
         if h == parts - 2:
             gather_relay(4)
+        if h == parts - 1:
+            gather_relay(5)
     even_hops(parts)
     odd_hops(parts, True)
-    dispatch(near[1])
-    gather_relay(5)
     odd_hops(parts, False)
     gather_finish(3)
     even_hops(parts + 1)
-    dispatch(near[2])
     odd_hops(parts + 1, False)
+    dispatch(far[0])
+    dispatch(far[1])
     drain(sums)
-    loads[7].wait()
-    loads[8].wait()
     gather_finish(4)
-    expert(near[1])
-    dispatch(near[3])
     gather_complete(3)
-    dense_up(near[1])
+    dense_up(far[0])
     gather_finish(5)
     gather_complete(4)
     gather_complete(5)
-    dense_down(to_stage(near[1]))
-    expert(near[2])
+    dense_down(to_stage(far[0]))
+    dense(far[1], to_stage(far[1]))
+    loads[7].wait()
+    loads[8].wait()
+    expert(far[0])
+    dispatch(far[2])
+    expert(far[1])
     dispatch(col)
-    send_on(near[1])
-    dense(near[2], to_stage(near[2]))
-    expert(near[3])
-    send_on(near[2])
-    dense(near[3], to_stage(near[3]))
-    sum_step(1, late[0], 0)
+    send_on(far[0])
+    dense(far[2], to_stage(far[2]))
+    dense(col, to_own)
+    sum_step(1, far[0], 0)
+    expert(far[2])
+    for h in range(1, parts - 1):
+        sum_step(1, far[0], h)
+    send_on(far[1])
+    sum_step(1, far[0], parts - 1)
     expert(col)
-    for h in range(1, parts - 1):
-        sum_step(1, late[0], h)
-    send_on(near[3])
-    sum_step(1, late[0], parts - 1)
-    dense(col, to_own)
-    sum_step(1, late[1], 0)
+    for h in range(parts // 2):
+        sum_step(1, far[1], h)
+    send_on(far[2])
+    for h in range(parts):
+        sum_step(1, far[2], h)
+    for h in range(parts // 2, parts):
+        sum_step(1, far[1], h)
     combine(col, True)
-    for h in range(1, parts + 1):
-        if h < parts:
-            sum_step(1, late[1], h)
-        sum_step(1, late[2], h - 1)
     for h in range(parts):
         sum_own(1, h)
         rows = rows_of(h)
         result[rows] = (hidden[rows].astype(f32) + own_sum[rows]).astype(result.dtype)
+        pltpu.make_async_copy(result.at[rows], result_out.at[rows], store_sem.at[h]).start()
     drain(sums)
     drain(finish)
+    for h in range(parts):
+        rows = rows_of(h)
+        pltpu.make_async_copy(result.at[rows], result_out.at[rows], store_sem.at[h]).wait()
 
 
 def fused_block(tokens, gain_one, qkv_part, out_part, gain_two, up_part, down_part, ids, first, second, capacity, heads):
@@ -900,7 +902,7 @@
     col_total = lax.axis_size("col")
     tok, model = tokens.shape
     parts = 4
-    hbm, vmem = pl.BlockSpec(memory_space=pl.ANY), pl.BlockSpec(memory_space=pltpu.VMEM)
+    hbm = pl.BlockSpec(memory_space=pl.ANY)
     bf16 = jnp.bfloat16
     three = qkv_part.shape[1]
     width = out_part.shape[0]
@@ -928,7 +930,7 @@
         pltpu.VMEM((tok, first.shape[1]), bf16),
         pltpu.VMEM((tok, up_part.shape[1]), bf16),
         pltpu.VMEM((col_total, 8, tok), jnp.int32),
-        dma((9,)),
+        dma((12,)),
         dma((2, col_total, parts, 2)),
         dma((2, col_total, parts)),
         dma((col_total, 2)),
@@ -941,15 +943,20 @@
         dma((col_total, row_total)),
         dma((col_total, row_total)),
         dma((col_total, row_total)),
+        pltpu.VMEM((1, model), jnp.float32),
+        pltpu.VMEM((1, model), jnp.float32),
+        pltpu.VMEM((1, tok), jnp.int32),
+        pltpu.VMEM((tok, model), bf16),
+        dma((parts,)),
     ]
     return pl.pallas_call(
         functools.partial(block_body, (row_total, col_total, capacity, heads, parts)),
         out_shape=jax.ShapeDtypeStruct((tok, model), bf16),
-        in_specs=[hbm, vmem, vmem, vmem] + [hbm] * 6,
-        out_specs=vmem,
+        in_specs=[hbm] * 10,
+        out_specs=hbm,
         scratch_shapes=scratch,
         compiler_params=pltpu.CompilerParams(
-            collective_id=0, has_side_effects=True, vmem_limit_bytes=62 * 2**20
+            collective_id=0, has_side_effects=True, vmem_limit_bytes=67043328
         ),
         name="block",
     )(

time: 183 us -> 172 us (0.940)
  Pallas kernels: 176 us -> 165 us
    pallas_call x1, Pallas kernels: 176 us -> 165 us  [fused_block(): pl.pallas_call(functools.partial(block_body, (row_total, col_total, capac...]
where the time goes in v3:
time: 172 us; the launch traced here: 169 us
  Pallas kernels  165 us (96%)
  local copies, waits for them, and re-layouts  4.23 us (2%)
    pallas_call x1, Pallas kernels, fused_block(): pl.pallas_call(functools.partial(block_body, (row_total, col_total, capac...  165 us

profile of v3, /device:TPU:6, one launch (start us, length us, event | category | flops | bytes accessed | tf_op | source)
XLA Modules:
  0.0 169.0 jit_solution(1105170875797984427)
XLA Ops:
  0.0 2.3 %reshape.15.refs_4_ = bf16[256,1536]{1,0:T(8,128)(2,1)} reshape(bf16[256,3,4,128]{3,2,1,0:T(4,128)(2,1)} %bitcast.8) | data formatting | bytes 1572864 | tf_op jit(solution)/shard_map/reshape | solution.py:1001
  2.3 164.7 %block.1 = bf16[128,2048]{1,0:T(8,128)(2,1)} custom-call(bf16[128,2048]{1,0:T(8,128)(2,1)} %refs_0_.1, f32[1,2048]{1,0:T(1,128)} %bitcast.9, f32[1,2048]{1,0:T(1,128)} %bitcast.10, s32[1,128]{1,0:T(1,128)} %bitcast.11, bf16[256,1536]{1,0:T(8,128)(2,1)} %reshape.15.refs_4_, bf16[512,256]{1,0:T(8,128)(2,1)} %refs_5_.1, bf16[256,2048]{1,0:T(8,128)(2,1)} %refs_6_.1, ...), custom_call_target="tpu_custom_call" | custom-call | tf_op jit(solution)/shard_map/block/pallas_call | solution.py:952
  167.1 1.9 %copy.12 = bf16[128,2048]{1,0:T(8,128)(2,1)} copy(bf16[128,2048]{1,0:T(8,128)(2,1)} %block.1) | data formatting | bytes 1048576
